TPU v7x, 32 devices: a whole 2x2x4 slice. The times are simulated.
32 devices in a mesh: groups: 2 (over x), section: 16 (over z, y, core).
Axes of the slice: x: 2, y: 2, z: 4, core: 2. Of those that a mesh axis runs over, the one named last changes fastest.
Arguments:
- tiles: float32 [32, 256, 256], P(('groups', 'section')), parts along dimension 0, may hold values from -6 to 6
- partners: int32 [32, 3], P(('groups', 'section')), parts along dimension 0, may hold values from 0 to 1, as said below
Outputs:
- shifts: float32 [32, 3, 9, 1024], P(('groups', 'section')), parts along dimension 0
There are 2 independent parts, one for each index of `groups`. A program takes and returns all parts, laid end to end along the dimension named above; each array names one. Nothing has to cross between parts.
Inputs may be any that keep to these rules, and one draw needn't show every extreme that they name: `partners`: every section lists at least one partner offset.
All inputs are finite; a program needn't handle non-finite values.
Results may differ from a plain program's by a relative error of at most 0.00007.
Values sent between devices are 32-bit elements; how exact they have to be, the bound alone decides.
No kernel may reach another device: no remote copies, remote signals or barrier semaphores. Data moves between devices by JAX's collectives and lax.ppermute only.
A program may use at most 64 MiB of HBM per device.

v0:
```python
import functools
import math

import jax
import jax.numpy as jnp
import numpy as np
from jax import lax
from jax.experimental import pallas as pl
from jax.experimental.pallas import tpu as pltpu
from jax.sharding import PartitionSpec as P

PATCH = 128
REACH = 3
CROP = 32
GRID = 3
HALF = PATCH // 2
SIDE = PATCH + HALF * (GRID - 1)
LANES = 512
ROWS = 144


def halves(table):
    top = table.astype(jnp.bfloat16)
    return top, (table - top.astype(np.float32)).astype(jnp.bfloat16)


def tables():
    y = np.arange(SIDE)
    freq = np.arange(HALF)
    first = np.zeros((SIDE, LANES))
    back = np.zeros((LANES, 128))
    shift = np.arange(CROP) - CROP // 2
    weight = np.where(freq == 0, 1.0, 2.0)
    for j in range(GRID):
        inside = ((y >= HALF * j) & (y < HALF * j + PATCH))[:, None]
        angle = 2 * math.pi * ((y[:, None] - HALF * j) * freq[None, :] % PATCH) / PATCH
        col = 256 * (j // 2) + HALF * (j % 2)
        first[:, col : col + HALF] = np.where(inside, np.cos(angle), 0)
        first[:, col + 128 : col + 128 + HALF] = np.where(inside, np.sin(angle), 0)
        ny = 256 + HALF + j
        first[:, ny] = np.where(inside[:, 0], 1.0 - 2.0 * (y % 2), 0)
        angle = 2 * math.pi * (freq[:, None] * shift[None, :] % PATCH) / PATCH
        out = slice(CROP * j, CROP * j + CROP)
        back[col : col + HALF, out] = weight[:, None] * np.cos(angle)
        back[col + 128 : col + 128 + HALF, out] = weight[:, None] * np.sin(angle)
        back[ny, out] = 1.0 - 2.0 * (shift % 2)
    x = np.arange(PATCH)
    angle = 2 * math.pi * (freq[:, None] * x[None, :] % PATCH) / PATCH
    second = np.zeros((ROWS, PATCH))
    second[:HALF] = np.cos(angle)
    second[HALF:PATCH] = np.sin(angle)
    second[PATCH] = 1.0 - 2.0 * (x % 2)
    angle = 2 * math.pi * (freq[None, :] * shift[:, None] % PATCH) / PATCH
    last = np.zeros((CROP, ROWS))
    last[:, :HALF] = weight * np.cos(angle)
    last[:, HALF:PATCH] = weight * np.sin(angle)
    last[:, PATCH] = 1.0 - 2.0 * (shift % 2)
    pick = np.zeros((SIDE, 128), np.float32)
    for j in range(GRID):
        pick[HALF * j : HALF * j + PATCH, CROP * j : CROP * j + CROP] = 1.0
    f_h, f_l = halves(first.astype(np.float32))
    s_h, s_l = halves(second.astype(np.float32))
    b_h, b_l = halves(back.astype(np.float32))
    l_h, l_l = halves(last.astype(np.float32))
    return (
        f_h,
        f_l,
        np.concatenate([s_h, s_h], axis=1),
        s_l,
        np.concatenate([b_h, b_l], axis=1),
        np.concatenate([l_h, l_l], axis=0),
        pick.astype(jnp.bfloat16),
    )


def mul(a, b):
    return jnp.dot(a, b, preferred_element_type=jnp.float32)


def split(x):
    top = x.astype(jnp.bfloat16)
    return top, (x - top.astype(jnp.float32)).astype(jnp.bfloat16)


def rows_of(tile, f_h, f_l):
    tile = tile - jnp.mean(tile)
    top, low = split(tile)
    segment = mul(top, f_h) + mul(low, f_h) + mul(top, f_l)
    return tile, split(segment)


def spread_of(tile, pick):
    square = tile * tile
    sums = []
    for values in (tile, square):
        for i in range(GRID):
            sums.append(jnp.sum(values[HALF * i : HALF * i + PATCH], axis=0, keepdims=True))
    sums.append(jnp.zeros((16 - len(sums), SIDE), jnp.float32))
    top, low = split(jnp.concatenate(sums, axis=0))
    means = (mul(top, pick) + mul(low, pick)) * (1.0 / PATCH**2)
    return [lax.rsqrt(means[GRID + i : GRID + i + 1] - means[i : i + 1] ** 2 + 1e-06) for i in range(GRID)]


def columns_of(segment, i, s_hh, s_l):
    top, low = (part[HALF * i : HALF * i + PATCH] for part in segment)
    return mul(s_hh, jnp.concatenate([top, low], axis=0)) + mul(s_l, top)


def power(a, b, sign):
    out = []
    for g in range(2):
        acc, acs, asc, ass = a(0, 2 * g), a(0, 2 * g + 1), a(1, 2 * g), a(1, 2 * g + 1)
        bcc, bcs, bsc, bss = b(0, 2 * g), b(0, 2 * g + 1), b(1, 2 * g), b(1, 2 * g + 1)
        anc, ans, bnc, bns = a(2, 2 * g), a(2, 2 * g + 1), b(2, 2 * g), b(2, 2 * g + 1)
        cc = (acc * bcc + asc * bsc) + (acs * bcs + ass * bss)
        ss = (acc * bss + ass * bcc) - (acs * bsc + asc * bcs)
        sc = (acs * bss - ass * bcs) + (acc * bsc - asc * bcc)
        cs = (acc * bcs - acs * bcc) + (asc * bss - ass * bsc)
        nc = anc * bnc + ans * bns
        ns = anc * bns - ans * bnc
        if sign < 0:
            sc, cs, ns = -sc, -cs, -ns
        zero = jnp.zeros_like(nc)
        out.append(jnp.concatenate([cc, sc, nc, zero], axis=0))
        out.append(jnp.concatenate([cs, ss, ns, zero], axis=0))
    return jnp.concatenate(out, axis=1)


def shifts_of(product, b_hl, l_hl):
    top, low = split(product)
    wide = mul(top, b_hl)
    half = wide[:, :128] + wide[:, 128:] + mul(low, b_hl[:, :128])
    top, low = split(half)
    wide = mul(l_hl, jnp.concatenate([top, low], axis=1))
    return wide[:CROP, :128] + wide[:CROP, 128:] + wide[CROP:, :128]


BANDS = ((0, HALF), (HALF, PATCH), (PATCH, PATCH + 8))


def own_kernel(tile, f_h, f_l, s_hh, s_l, pick, spec, spread):
    values, segment = rows_of(tile[...], f_h[...], f_l[...])
    lane = lax.broadcasted_iota(jnp.int32, (8, LANES), 1)
    row = lax.broadcasted_iota(jnp.int32, (8, LANES), 0)
    constant = (row == 0) & ((lane == 0) | (lane == HALF) | (lane == 256))
    for i in range(GRID):
        part = columns_of(segment, i, s_hh[...], s_l[...])
        spec[i] = part
        spec[i, 0:8, :] = jnp.where(constant, 0.0, part[0:8])
    for i, value in enumerate(spread_of(values, pick[...])):
        spread[i : i + 1, :] = value


def pair_kernel(sign, tile, spec, spread, f_h, f_l, s_hh, s_l, b_hl, l_hl, pick, out):
    values, segment = rows_of(tile[...], f_h[...], f_l[...])
    other = spread_of(values, pick[...])
    for i in range(GRID):
        part = columns_of(segment, i, s_hh[...], s_l[...])
        own = lambda r, c, i=i: spec[i, BANDS[r][0] : BANDS[r][1], 128 * c : 128 * c + 128]
        new = lambda r, c, part=part: part[BANDS[r][0] : BANDS[r][1], 128 * c : 128 * c + 128]
        result = shifts_of(power(own, new, sign), b_hl[...], l_hl[...])
        scale = spread[i : i + 1, :] * other[i] * (1.0 / float(PATCH**3))
        out[i] = result * scale


def call(kernel, outs, *args):
    vmem = pl.BlockSpec(memory_space=pltpu.VMEM)
    return pl.pallas_call(
        kernel,
        out_shape=outs,
        in_specs=[vmem] * len(args),
        out_specs=jax.tree.map(lambda _: vmem, outs),
        cost_estimate=pl.CostEstimate(flops=4_000_000_000, bytes_accessed=2_000_000, transcendentals=0),
    )(*args)


def body(tiles, partners):
    f_h, f_l, s_hh, s_l, b_hl, l_hl, pick = (jnp.asarray(t) for t in tables())
    total = lax.axis_size("section")
    position = lax.axis_index("section")
    even = position % 2 == 0
    send = functools.partial(lax.ppermute, axis_name="section")
    ahead = [(i, i + (1 if i % 2 == 0 else 3)) for i in range(total)]
    ahead = [(i, j) for i, j in ahead if j < total]
    swap = [(i, i ^ 1) for i in range(total)]
    direct = send(tiles, perm=[(i, i - 2) for i in range(2, total)])
    early = send(tiles, perm=ahead)
    relay = send(direct, perm=swap)
    spec, spread = call(
        own_kernel,
        (jax.ShapeDtypeStruct((GRID, ROWS, LANES), jnp.float32), jax.ShapeDtypeStruct((8, 128), jnp.float32)),
        tiles[0], f_h, f_l, s_hh, s_l, pick,
    )
    block = jax.ShapeDtypeStruct((GRID, CROP, 128), jnp.float32)

    def pair(tile, sign):
        return call(functools.partial(pair_kernel, sign), block, tile[0], spec, spread, f_h, f_l, s_hh, s_l, b_hl, l_hl, pick)

    back = send(pair(early, -1), perm=[(j, i) for i, j in ahead])
    second = pair(direct, 1)
    third = pair(relay, 1)
    result = jnp.stack([jnp.where(even, back, third), second, jnp.where(even, third, back)])
    result = result[..., : GRID * CROP].reshape(REACH, GRID, CROP, GRID, CROP).transpose(0, 1, 3, 2, 4)
    result = result.reshape(REACH, GRID * GRID, CROP * CROP)
    offsets = jnp.arange(REACH, dtype=jnp.int32) + 1
    listed = (partners[0] == 1) & (position + offsets < total)
    return jnp.where(listed[:, None, None], result, 0.0)[None]


def solution(mesh):
    in_specs = (P(("groups", "section"), None, None), P(("groups", "section"), None))
    out_specs = P(("groups", "section"), None, None, None)
    return jax.shard_map(body, mesh=mesh, in_specs=in_specs, out_specs=out_specs, check_vma=False)
```

profile of v0, /device:TPU:17, one launch (start us, length us, event | category | flops | bytes accessed | tf_op | source)
XLA Modules:
  0.0 28.6 jit_solution(16058271429722775426)
XLA Ops:
  0.0 3.8 %collective-permute-start = (f32[1,256,256]{2,1,0:T(8,128)}, f32[1,256,256]{2,1,0:T(8,128)S(1)}, u32[]{:S(2)}, u32[]{:S(2)}) collective-permute-start(f32[1,256,256]{2,1,0:T(8,128)} %param.9), channel_id=1, source_target_pairs={{0,1},{1,4},{2,3},{3,6},{4,5},{5,8},{6,7},{7,10},{8,9},{9,12},{10,... | collective-permute-start | bytes 786440 | tf_op jit(solution)/shard_map/ppermute | solution.py:187
  3.8 3.0 %collective-permute-start.2 = (f32[1,256,256]{2,1,0:T(8,128)}, f32[1,256,256]{2,1,0:T(8,128)S(1)}, u32[]{:S(2)}, u32[]{:S(2)}) collective-permute-start(f32[1,256,256]{2,1,0:T(8,128)} %param.9), channel_id=1, source_target_pairs={{2,0},{3,1},{4,2},{5,3},{6,4},{7,5},{8,6},{9,7},{10,8},{11,9},{12,... | collective-permute-start | bytes 786440 | tf_op jit(solution)/shard_map/ppermute | solution.py:186
  6.8 3.0 %shard_map.91 = (f32[3,144,512]{2,1,0:T(8,128)}, f32[8,128]{1,0:T(8,128)}) custom-call(f32[256,256]{1,0:T(8,128)} %bitcast.20, bf16[256,512]{1,0:T(8,128)(2,1)} %constant.37.clone.f_h, bf16[256,512]{1,0:T(8,128)(2,1)} %constant.38.clone.f_l, bf16[144,256]{1,0:T(8,128)(2,1)} %constant.39.clone.s_hh, bf16[144,128]{1,0:T(8,128)(2,1)} %constant.40.clone.s_l, ...), custom_call_target="tpu_custom_call" | custom-call | flops 4000000000 | bytes 2000000 | tf_op jit(solution)/shard_map/pallas_call | solution.py:168
  9.8 0.0 copy-start.4
  9.8 0.7 %copy-done.4 = s32[1,3]{1,0:T(1,128)S(1)} copy-done((s32[1,3]{1,0:T(1,128)S(1)}, s32[1,3]{1,0:T(1,128)}, u32[]{:S(2)}) %copy-start.4) | copy-done | bytes 36
  10.4 0.0 collective-permute-done
  10.4 0.0 copy-start.2
  10.5 0.7 %copy-done.2 = f32[1,256,256]{2,1,0:T(8,128)} copy-done((f32[1,256,256]{2,1,0:T(8,128)}, f32[1,256,256]{2,1,0:T(8,128)S(1)}, u32[]{:S(2)}) %copy-start.2) | copy-done | bytes 262168
  11.2 4.0 %shard_map.92 = f32[3,32,128]{2,1,0:T(8,128)} custom-call(f32[256,256]{1,0:T(8,128)} %bitcast.22, f32[3,144,512]{2,1,0:T(8,128)} %get-tuple-element.7.spec, f32[8,128]{1,0:T(8,128)} %get-tuple-element.8.spread, bf16[256,512]{1,0:T(8,128)(2,1)} %constant.37.clone.f_h, bf16[256,512]{1,0:T(8,128)(2,1)} %constant.38.clone.f_l, ...), custom_call_target="tpu_custom_call" | custom-call | flops 4000000000 | bytes 2000000 | tf_op jit(solution)/shard_map/pallas_call | solution.py:168
  15.1 1.9 %collective-permute-start.1 = (f32[3,32,128]{2,1,0:T(8,128)}, f32[3,32,128]{2,1,0:T(8,128)S(1)}, u32[]{:S(2)}, u32[]{:S(2)}) collective-permute-start(f32[3,32,128]{2,1,0:T(8,128)} %shard_map.92), channel_id=1, source_target_pairs={{1,0},{4,1},{3,2},{6,3},{5,4},{8,5},{7,6},{10,7},{9,8},{12,9},{11,... | collective-permute-start | bytes 147464 | tf_op jit(solution)/shard_map/ppermute | solution.py:199
  17.0 0.0 collective-permute-done.2
  17.0 0.0 copy-start.1
  17.0 0.6 %collective-permute-start.3 = (f32[1,256,256]{2,1,0:T(8,128)S(1)}, f32[1,256,256]{2,1,0:T(8,128)S(1)}, u32[]{:S(2)}, u32[]{:S(2)}) collective-permute-start(f32[1,256,256]{2,1,0:T(8,128)S(1)} %collective-permute-done.2), channel_id=1, source_target_pairs={{0,1},{1,0},{2,3},{3,2},{4,5},{5,4},{6,7},{7,6},{8,9},{9,8},{10,11... | collective-permute-start | bytes 786440 | tf_op jit(solution)/shard_map/ppermute | solution.py:188
  17.6 0.1 copy-done.1
  17.7 3.9 %shard_map.94 = f32[3,32,128]{2,1,0:T(8,128)} custom-call(f32[256,256]{1,0:T(8,128)} %bitcast.21, f32[3,144,512]{2,1,0:T(8,128)} %get-tuple-element.7.spec, f32[8,128]{1,0:T(8,128)} %get-tuple-element.8.spread, bf16[256,512]{1,0:T(8,128)(2,1)} %constant.37.clone.f_h, bf16[256,512]{1,0:T(8,128)(2,1)} %constant.38.clone.f_l, ...), custom_call_target="tpu_custom_call" | custom-call | flops 4000000000 | bytes 2000000 | tf_op jit(solution)/shard_map/pallas_call | solution.py:168
  21.7 0.0 collective-permute-done.3
  21.7 0.0 copy-start.3
  21.7 0.7 %copy-done.3 = f32[1,256,256]{2,1,0:T(8,128)} copy-done((f32[1,256,256]{2,1,0:T(8,128)}, f32[1,256,256]{2,1,0:T(8,128)S(1)}, u32[]{:S(2)}) %copy-start.3) | copy-done | bytes 262168
  22.4 3.9 %shard_map.93 = f32[3,32,128]{2,1,0:T(8,128)} custom-call(f32[256,256]{1,0:T(8,128)} %bitcast.23, f32[3,144,512]{2,1,0:T(8,128)} %get-tuple-element.7.spec, f32[8,128]{1,0:T(8,128)} %get-tuple-element.8.spread, bf16[256,512]{1,0:T(8,128)(2,1)} %constant.37.clone.f_h, bf16[256,512]{1,0:T(8,128)(2,1)} %constant.38.clone.f_l, ...), custom_call_target="tpu_custom_call" | custom-call | flops 4000000000 | bytes 2000000 | tf_op jit(solution)/shard_map/pallas_call | solution.py:168
  26.3 0.0 copy-start
  26.3 0.0 collective-permute-done.1
  26.3 0.8 %select_bitcast_fusion.1 = (f32[1,3,32,128]{3,2,1,0:T(8,128)S(1)}, f32[1,3,32,128]{3,2,1,0:T(8,128)S(1)}) fusion(f32[3,32,128]{2,1,0:T(8,128)S(1)} %collective-permute-done.1, f32[3,32,128]{2,1,0:T(8,128)} %shard_map.93, pred[]{:T(512)S(6)} %eq.17), kind=kLoop, calls=%fused_computation.4 | loop fusion | flops 24576 | bytes 196609 | tf_op jit(solution)/shard_map/stack | solution.py:202
  27.2 0.0 copy-done
  27.2 0.2 reshape.30
  27.5 0.2 reshape.31
  27.7 0.1 broadcast_select_fusion
  27.8 0.8 %copy.12 = f32[1,3,9,1024]{3,0,2,1:T(1,128)} copy(f32[1,3,9,1024]{3,1,2,0:T(4,128)S(1)} %broadcast_select_fusion) | data formatting | bytes 221184 | tf_op jit(solution)/shard_map/jit(_where)/select_n | solution.py:207
  (3 shorter events, 0.1 us)
Async XLA Ops:
  0.0 10.4 %collective-permute-start = (f32[1,256,256]{2,1,0:T(8,128)}, f32[1,256,256]{2,1,0:T(8,128)S(1)}, u32[]{:S(2)}, u32[]{:S(2)}) collective-permute-start(f32[1,256,256]{2,1,0:T(8,128)} %param.9), channel_id=1, source_target_pairs={{0,1},{1,4},{2,3},{3,6},{4,5},{5,8},{6,7},{7,10},{8,9},{9,12},{10,... | collective-permute-start | bytes 786440 | tf_op jit(solution)/shard_map/ppermute | solution.py:187
  3.8 13.3 %collective-permute-start.2 = (f32[1,256,256]{2,1,0:T(8,128)}, f32[1,256,256]{2,1,0:T(8,128)S(1)}, u32[]{:S(2)}, u32[]{:S(2)}) collective-permute-start(f32[1,256,256]{2,1,0:T(8,128)} %param.9), channel_id=1, source_target_pairs={{2,0},{3,1},{4,2},{5,3},{6,4},{7,5},{8,6},{9,7},{10,8},{11,9},{12,... | collective-permute-start | bytes 786440 | tf_op jit(solution)/shard_map/ppermute | solution.py:186
  9.8 0.7 %copy-start.4 = (s32[1,3]{1,0:T(1,128)S(1)}, s32[1,3]{1,0:T(1,128)}, u32[]{:S(2)}) copy-start(s32[1,3]{1,0:T(1,128)} %param.10) | copy-start | bytes 40
  10.4 0.7 %copy-start.2 = (f32[1,256,256]{2,1,0:T(8,128)}, f32[1,256,256]{2,1,0:T(8,128)S(1)}, u32[]{:S(2)}) copy-start(f32[1,256,256]{2,1,0:T(8,128)S(1)} %collective-permute-done) | copy-start | bytes 786436
  15.1 11.2 %collective-permute-start.1 = (f32[3,32,128]{2,1,0:T(8,128)}, f32[3,32,128]{2,1,0:T(8,128)S(1)}, u32[]{:S(2)}, u32[]{:S(2)}) collective-permute-start(f32[3,32,128]{2,1,0:T(8,128)} %shard_map.92), channel_id=1, source_target_pairs={{1,0},{4,1},{3,2},{6,3},{5,4},{8,5},{7,6},{10,7},{9,8},{12,9},{11,... | collective-permute-start | bytes 147464 | tf_op jit(solution)/shard_map/ppermute | solution.py:199
  17.0 0.7 %copy-start.1 = (f32[1,256,256]{2,1,0:T(8,128)}, f32[1,256,256]{2,1,0:T(8,128)S(1)}, u32[]{:S(2)}) copy-start(f32[1,256,256]{2,1,0:T(8,128)S(1)} %collective-permute-done.2) | copy-start | bytes 786436
  17.0 4.6 %collective-permute-start.3 = (f32[1,256,256]{2,1,0:T(8,128)S(1)}, f32[1,256,256]{2,1,0:T(8,128)S(1)}, u32[]{:S(2)}, u32[]{:S(2)}) collective-permute-start(f32[1,256,256]{2,1,0:T(8,128)S(1)} %collective-permute-done.2), channel_id=1, source_target_pairs={{0,1},{1,0},{2,3},{3,2},{4,5},{5,4},{6,7},{7,6},{8,9},{9,8},{10,11... | collective-permute-start | bytes 786440 | tf_op jit(solution)/shard_map/ppermute | solution.py:188
  21.7 0.7 %copy-start.3 = (f32[1,256,256]{2,1,0:T(8,128)}, f32[1,256,256]{2,1,0:T(8,128)S(1)}, u32[]{:S(2)}) copy-start(f32[1,256,256]{2,1,0:T(8,128)S(1)} %collective-permute-done.3) | copy-start | bytes 786436
  26.3 0.8 %copy-start = (f32[3,32,128]{2,1,0:T(8,128)S(1)}, f32[3,32,128]{2,1,0:T(8,128)}, u32[]{:S(2)}) copy-start(f32[3,32,128]{2,1,0:T(8,128)} %shard_map.94) | copy-start | bytes 147460
where the time goes:
time: 28.9 us; the launch traced here: 28.6 us
  Pallas kernels  14.8 us (51%)
  starting transfers between devices  9.31 us (32%)
  local copies, waits for them, and re-layouts  3.44 us (12%)
  other arithmetic  0.94 us (3%)
    pallas_call x4, Pallas kernels, call(): pl.pallas_call(kernel, out_shape=outs, in_specs=[vmem] * len(args), out_s...  14.8 us
    ppermute x1, starting transfers between devices, body(): early = send(tiles, perm=ahead)  3.75 us
    ppermute x1, starting transfers between devices, body(): direct = send(tiles, perm=[(i, i - 2) for i in range(2, total)])  3.03 us
    unnamed x10, local copies, waits for them, and re-layouts  2.15 us
    ppermute x1, starting transfers between devices, body(): back = send(pair(early, -1), perm=[(j, i) for i, j in ahead])  1.91 us
    another operation x2, other arithmetic, body(): jnp.stack([jnp.where(even, back, third), second, jnp.where(even, third, b...  0.83 us
    select_n x1, local copies, waits for them, and re-layouts, body(): return jnp.where(listed[:, None, None], result, 0.0)[None]  0.76 us
    ppermute x1, starting transfers between devices, body(): relay = send(direct, perm=swap)  0.61 us
  transfers between devices with their start and end apart: 4, of which 0 were waited for; matrix products, arithmetic and copies ran while one was open for 0% of the time, Pallas kernels for 52%

commit v1 on v0

v1 whole, which is shorter than its diff:
```python
import functools
import math

import jax
import jax.numpy as jnp
import numpy as np
from jax import lax
from jax.experimental import pallas as pl
from jax.experimental.pallas import tpu as pltpu
from jax.sharding import PartitionSpec as P


PATCH = 128
REACH = 3
CROP = 32
GRID = 3
HALF = PATCH // 2
SIDE = PATCH + HALF * (GRID - 1)
LANES = 512
ROWS = 144


PLACES = {
    "first_h": (slice(0, SIDE), slice(0, LANES)),
    "first_l": (slice(SIDE, 2 * SIDE), slice(0, LANES)),
    "back": (slice(512, 1024), slice(0, 256)),
    "second": (slice(512, 656), slice(256, 512)),
    "second_l": (slice(656, 800), slice(256, 384)),
    "last": (slice(912, 976), slice(256, 400)),
    "pick": (slice(656, 912), slice(384, 512)),
}


def halves(table):
    top = table.astype(jnp.bfloat16)
    return top, (table - top.astype(np.float32)).astype(jnp.bfloat16)


def tables():
    y = np.arange(SIDE)
    freq = np.arange(HALF)
    first = np.zeros((SIDE, LANES))
    back = np.zeros((LANES, 128))
    shift = np.arange(CROP) - CROP // 2
    weight = np.where(freq == 0, 1.0, 2.0)
    for j in range(GRID):
        inside = ((y >= HALF * j) & (y < HALF * j + PATCH))[:, None]
        angle = 2 * math.pi * ((y[:, None] - HALF * j) * freq[None, :] % PATCH) / PATCH
        col = 256 * (j // 2) + HALF * (j % 2)
        first[:, col : col + HALF] = np.where(inside, np.cos(angle), 0)
        first[:, col + 128 : col + 128 + HALF] = np.where(inside, np.sin(angle), 0)
        ny = 256 + HALF + j
        first[:, ny] = np.where(inside[:, 0], 1.0 - 2.0 * (y % 2), 0)
        angle = 2 * math.pi * (freq[:, None] * shift[None, :] % PATCH) / PATCH
        out = slice(CROP * j, CROP * j + CROP)
        back[col : col + HALF, out] = weight[:, None] * np.cos(angle)
        back[col + 128 : col + 128 + HALF, out] = weight[:, None] * np.sin(angle)
        back[ny, out] = 1.0 - 2.0 * (shift % 2)
    x = np.arange(PATCH)
    angle = 2 * math.pi * (freq[:, None] * x[None, :] % PATCH) / PATCH
    second = np.zeros((ROWS, PATCH))
    second[:HALF] = np.cos(angle)
    second[HALF:PATCH] = np.sin(angle)
    second[PATCH] = 1.0 - 2.0 * (x % 2)
    angle = 2 * math.pi * (freq[None, :] * shift[:, None] % PATCH) / PATCH
    last = np.zeros((CROP, ROWS))
    last[:, :HALF] = weight * np.cos(angle)
    last[:, HALF:PATCH] = weight * np.sin(angle)
    last[:, PATCH] = 1.0 - 2.0 * (shift % 2)
    pick = np.zeros((SIDE, 128), np.float32)
    for j in range(GRID):
        pick[HALF * j : HALF * j + PATCH, CROP * j : CROP * j + CROP] = 1.0
    packed = np.zeros((1024, LANES), np.float32)
    f_h, f_l = halves(first.astype(np.float32))
    s_h, s_l = halves(second.astype(np.float32))
    b_h, b_l = halves(back.astype(np.float32))
    l_h, l_l = halves(last[[4 * q + r for r in range(4) for q in range(CROP // 4)]].astype(np.float32))
    for (rows, cols), table in zip(
        PLACES.values(),
        (
            f_h,
            f_l,
            np.concatenate([b_h, b_l], axis=1),
            np.concatenate([s_h, s_h], axis=1),
            s_l,
            np.concatenate([l_h, l_l], axis=0),
            pick,
        ),
        strict=True,
    ):
        packed[rows, cols] = table
    return packed.astype(jnp.bfloat16)


def mul(a, b):
    return jnp.dot(a, b, preferred_element_type=jnp.float32)


def split(x):
    top = x.astype(jnp.bfloat16)
    return top, (x - top.astype(jnp.float32)).astype(jnp.bfloat16)


def rows_of(tile, table):
    tile = tile - jnp.mean(tile)
    top, low = split(tile)
    first = table("first_h")
    return tile, split(mul(top, first) + mul(low, first) + mul(top, table("first_l")))


def spread_of(tile, table):
    square = tile * tile
    sums = []
    for values in (tile, square):
        for i in range(GRID):
            sums.append(jnp.sum(values[HALF * i : HALF * i + PATCH], axis=0, keepdims=True))
    sums.append(jnp.zeros((16 - len(sums), SIDE), jnp.float32))
    top, low = split(jnp.concatenate(sums, axis=0))
    means = (mul(top, table("pick")) + mul(low, table("pick"))) * (1.0 / PATCH**2)
    return [lax.rsqrt(means[GRID + i : GRID + i + 1] - means[i : i + 1] ** 2 + 1e-06) for i in range(GRID)]


def columns_of(segment, i, table):
    top, low = (part[HALF * i : HALF * i + PATCH] for part in segment)
    return mul(table("second"), jnp.concatenate([top, low], axis=0)) + mul(table("second_l"), top)


def power(a, b):
    out = []
    for g in range(2):
        acc, acs, asc, ass = a(0, 2 * g), a(0, 2 * g + 1), a(1, 2 * g), a(1, 2 * g + 1)
        bcc, bcs, bsc, bss = b(0, 2 * g), b(0, 2 * g + 1), b(1, 2 * g), b(1, 2 * g + 1)
        anc, ans, bnc, bns = a(2, 2 * g), a(2, 2 * g + 1), b(2, 2 * g), b(2, 2 * g + 1)
        cc = (acc * bcc + asc * bsc) + (acs * bcs + ass * bss)
        ss = (acc * bss + ass * bcc) - (acs * bsc + asc * bcs)
        sc = (acs * bss - ass * bcs) + (acc * bsc - asc * bcc)
        cs = (acc * bcs - acs * bcc) + (asc * bss - ass * bsc)
        nc = anc * bnc + ans * bns
        ns = anc * bns - ans * bnc
        zero = jnp.zeros_like(nc)
        out.append(jnp.concatenate([cc, sc, nc, zero], axis=0))
        out.append(jnp.concatenate([cs, ss, ns, zero], axis=0))
    return jnp.concatenate(out, axis=1)


def shifts_of(products, table):
    parts = [split(product) for product in products]
    count = len(parts)
    wide = mul(jnp.concatenate([top for top, _ in parts] + [low for _, low in parts], axis=0), table("back"))
    out = []
    for i in range(count):
        top, low = (wide[ROWS * k : ROWS * k + ROWS] for k in (i, count + i))
        top, low = split((top[:, :128] + top[:, 128:]) + (low[:, :128] + low[:, 128:]))
        ends = mul(table("last"), jnp.concatenate([top, low], axis=1))
        out.append(ends[:CROP, :128] + ends[:CROP, 128:] + (ends[CROP:, :128] + ends[CROP:, 128:]))
    return out


def patches_of(block):
    lane = lax.broadcasted_iota(jnp.int32, (8, 128), 1) // CROP
    rows = [block[8 * r : 8 * r + 8] for r in range(4)]
    out = []
    for j in range(GRID):
        moved = [rows[r] if r == j else pltpu.roll(rows[r], CROP * ((r - j) % 4), 1) for r in range(4)]
        out.append(jnp.where(lane < 2, jnp.where(lane == 0, moved[0], moved[1]), jnp.where(lane == 2, moved[2], moved[3])))
    return out


BANDS = ((0, HALF), (HALF, PATCH), (PATCH, PATCH + 8))


def reader(packed):
    return lambda name: packed[PLACES[name][0], PLACES[name][1]]


def own_kernel(tile, packed, spec, spread):
    table = reader(packed)
    values, segment = rows_of(tile[...], table)
    lane = lax.broadcasted_iota(jnp.int32, (8, LANES), 1)
    row = lax.broadcasted_iota(jnp.int32, (8, LANES), 0)
    constant = (row == 0) & ((lane == 0) | (lane == HALF) | (lane == 256))
    for i in range(GRID):
        part = columns_of(segment, i, table)
        spec[i] = part
        spec[i, 0:8, :] = jnp.where(constant, 0.0, part[0:8])
    for i, value in enumerate(spread_of(values, table)):
        spread[i : i + 1, :] = value


def pair(tile, spec, spread, packed):
    table = reader(packed)
    values, segment = rows_of(tile[...], table)
    other = spread_of(values, table)
    products = []
    for i in range(GRID):
        part = columns_of(segment, i, table)
        own = lambda r, c, i=i: spec[i, BANDS[r][0] : BANDS[r][1], 128 * c : 128 * c + 128]
        new = lambda r, c, part=part: part[BANDS[r][0] : BANDS[r][1], 128 * c : 128 * c + 128]
        products.append(power(own, new))
    out = []
    for i, block in enumerate(shifts_of(products, table)):
        out += patches_of(block * (spread[i : i + 1, :] * other[i] * (1.0 / float(PATCH**3))))
    return out


def pair_kernel(tile, spec, spread, packed, out):
    for p, block in enumerate(pair(tile, spec, spread, packed)):
        out[8 * p : 8 * p + 8, :] = block


def final_kernel(partners, tile, spec, spread, packed, second, third, out, turned):
    position = lax.axis_index("section")
    total = lax.axis_size("section")
    even = position % 2 == 0

    def place(slot, p, value):
        turned[slot, pl.ds(p, 8, stride=16), :] = value

    listed = [(partners[0, slot] == 1) & (position + (slot + 1) < total) for slot in range(REACH)]
    for p in range(GRID * GRID):
        place(1, p, jnp.where(listed[1], second[8 * p : 8 * p + 8, :], 0.0))
    for p, value in enumerate(pair(tile, spec, spread, packed)):
        passed = third[8 * p : 8 * p + 8, :]
        place(0, p, jnp.where(listed[0], jnp.where(even, value, passed), 0.0))
        place(2, p, jnp.where(listed[2], jnp.where(even, passed, value), 0.0))
    for slot in range(REACH):
        for q in range(8):
            out[0, slot, 0:8, 128 * q : 128 * q + 128] = turned[slot, 16 * q : 16 * q + 8, :]
            out[0, slot, 8:9, 128 * q : 128 * q + 128] = turned[slot, 16 * q + 8 : 16 * q + 9, :]


def call(kernel, outs, *args, scalars=0, scratch=()):
    vmem = pl.BlockSpec(memory_space=pltpu.VMEM)
    smem = pl.BlockSpec(memory_space=pltpu.SMEM)
    return pl.pallas_call(
        kernel,
        out_shape=outs,
        in_specs=[smem] * scalars + [vmem] * (len(args) - scalars),
        out_specs=jax.tree.map(lambda _: vmem, outs),
        scratch_shapes=scratch,
        compiler_params=pltpu.CompilerParams(vmem_limit_bytes=16 * 1024 * 1024),
        cost_estimate=pl.CostEstimate(flops=4_000_000_000, bytes_accessed=2_000_000, transcendentals=0),
    )(*args)


def body(tiles, partners):
    packed = jnp.asarray(tables())
    total = lax.axis_size("section")
    send = functools.partial(lax.ppermute, axis_name="section")
    near = [(i, i - (1 if i % 2 else 3)) for i in range(total)]
    near = [(i, j) for i, j in near if j >= 0]
    spectra = (jax.ShapeDtypeStruct((GRID, ROWS, LANES), jnp.float32), jax.ShapeDtypeStruct((8, 128), jnp.float32))
    block = jax.ShapeDtypeStruct((8 * GRID * GRID, 128), jnp.float32)
    direct = send(tiles, perm=[(i, i - 2) for i in range(2, total)])
    early = send(tiles, perm=near)
    relay = send(direct, perm=[(i, i ^ 1) for i in range(total)])
    spec, spread = call(own_kernel, spectra, tiles[0], packed)
    second = call(pair_kernel, block, direct[0], spec, spread, packed)
    third = call(pair_kernel, block, relay[0], spec, spread, packed)
    return call(
        final_kernel,
        jax.ShapeDtypeStruct((1, REACH, GRID * GRID, CROP * CROP), jnp.float32),
        partners, early[0], spec, spread, packed, second, third,
        scalars=1,
        scratch=[pltpu.VMEM((REACH, 128, 128), jnp.float32)],
    )


def solution(mesh):
    in_specs = (P(("groups", "section"), None, None), P(("groups", "section"), None))
    out_specs = P(("groups", "section"), None, None, None)
    return jax.shard_map(body, mesh=mesh, in_specs=in_specs, out_specs=out_specs, check_vma=False)
```

time: 28.9 us -> 18.5 us (0.64)
  the two profiles are of different devices: /device:TPU:17 before, /device:TPU:13 now
where the time goes in v1:
time: 18.5 us; the launch traced here: 18.3 us
  starting transfers between devices  6.52 us (35%)
  Pallas kernels  6.02 us (33%)
  local copies, waits for them, and re-layouts  3.58 us (19%)
  waiting for transfers between devices  2.1 us (11%)
    pallas_call x4, Pallas kernels, call(): pl.pallas_call(kernel, out_shape=outs, in_specs=[smem] * scalars + [vmem]...  6.02 us
    ppermute x1, starting transfers between devices, body(): early = send(tiles, perm=near)  2.86 us
    unnamed x8, local copies, waits for them, and re-layouts  2.82 us
    ppermute x1, starting transfers between devices, body(): direct = send(tiles, perm=[(i, i - 2) for i in range(2, total)])  2.12 us
    ppermute x1, waiting for transfers between devices, body(): direct = send(tiles, perm=[(i, i - 2) for i in range(2, total)])  2.1 us
    ppermute x1, starting transfers between devices, body(): relay = send(direct, perm=[(i, i ^ 1) for i in range(total)])  1.53 us
    pallas_call x1, local copies, waits for them, and re-layouts, call(): pl.pallas_call(kernel, out_shape=outs, in_specs=[smem] * scalars + [vmem]...  0.76 us
  transfers between devices with their start and end apart: 3, of which 1 were waited for; matrix products, arithmetic and copies ran while one was open for 0% of the time, Pallas kernels for 22%

profile of v1, /device:TPU:13, one launch (start us, length us, event | category | flops | bytes accessed | tf_op | source)
XLA Modules:
  0.0 18.3 jit_solution(18092919399180924557)
XLA Ops:
  0.0 2.1 %collective-permute-start.1 = (f32[1,256,256]{2,1,0:T(8,128)}, f32[1,256,256]{2,1,0:T(8,128)S(1)}, u32[]{:S(2)}, u32[]{:S(2)}) collective-permute-start(f32[1,256,256]{2,1,0:T(8,128)} %param.3), channel_id=1, source_target_pairs={{2,0},{3,1},{4,2},{5,3},{6,4},{7,5},{8,6},{9,7},{10,8},{11,9},{12,... | collective-permute-start | bytes 786440 | tf_op jit(solution)/shard_map/ppermute | solution.py:254
  2.1 2.9 %collective-permute-start = (f32[1,256,256]{2,1,0:T(8,128)}, f32[1,256,256]{2,1,0:T(8,128)S(1)}, u32[]{:S(2)}, u32[]{:S(2)}) collective-permute-start(f32[1,256,256]{2,1,0:T(8,128)} %param.3), channel_id=1, source_target_pairs={{1,0},{3,2},{4,1},{5,4},{6,3},{7,6},{8,5},{9,8},{10,7},{11,10},{12... | collective-permute-start | bytes 786440 | tf_op jit(solution)/shard_map/ppermute | solution.py:255
  5.0 0.0 copy-start
  5.0 0.9 %copy-done = f32[1,256,256]{2,1,0:T(8,128)S(1)} copy-done((f32[1,256,256]{2,1,0:T(8,128)S(1)}, f32[1,256,256]{2,1,0:T(8,128)}, u32[]{:S(2)}) %copy-start) | copy-done | bytes 262168
  6.0 0.0 copy-start.2
  6.0 1.2 %copy-done.2 = bf16[1024,512]{1,0:T(8,128)(2,1)S(1)} copy-done((bf16[1024,512]{1,0:T(8,128)(2,1)S(1)}, bf16[1024,512]{1,0:T(8,128)(2,1)}, u32[]{:S(2)}) %copy-start.2) | copy-done | bytes 1048600
  7.2 0.0 copy-start.3
  7.2 0.9 %shard_map.37 = (f32[3,144,512]{2,1,0:T(8,128)S(1)}, f32[8,128]{1,0:T(8,128)S(1)}) custom-call(f32[256,256]{1,0:T(8,128)S(1)} %bitcast.4, bf16[1024,512]{1,0:T(8,128)(2,1)S(1)} %copy-done.2), custom_call_target="tpu_custom_call" | custom-call | flops 4000000000 | bytes 2000000 | tf_op jit(solution)/shard_map/pallas_call | solution.py:235
  8.1 2.1 %collective-permute-done.1 = f32[1,256,256]{2,1,0:T(8,128)S(1)} collective-permute-done((f32[1,256,256]{2,1,0:T(8,128)}, f32[1,256,256]{2,1,0:T(8,128)S(1)}, u32[]{:S(2)}, u32[]{:S(2)}) %collective-permute-start.1) | collective-permute-done | bytes 262176 | tf_op jit(solution)/shard_map/ppermute | solution.py:254
  10.2 1.5 %collective-permute-start.2 = (f32[1,256,256]{2,1,0:T(8,128)S(1)}, f32[1,256,256]{2,1,0:T(8,128)S(1)}, u32[]{:S(2)}, u32[]{:S(2)}) collective-permute-start(f32[1,256,256]{2,1,0:T(8,128)S(1)} %collective-permute-done.1), channel_id=1, source_target_pairs={{0,1},{1,0},{2,3},{3,2},{4,5},{5,4},{6,7},{7,6},{8,9},{9,8},{10,11... | collective-permute-start | bytes 786440 | tf_op jit(solution)/shard_map/ppermute | solution.py:256
  11.7 0.0 copy-done.3
  11.7 1.5 %shard_map.38.second = f32[72,128]{1,0:T(8,128)S(1)} custom-call(f32[256,256]{1,0:T(8,128)S(1)} %bitcast.6, f32[3,144,512]{2,1,0:T(8,128)S(1)} %get-tuple-element.7.spec, f32[8,128]{1,0:T(8,128)S(1)} %get-tuple-element.8.spread, bf16[1024,512]{1,0:T(8,128)(2,1)S(1)} %copy-done.3), custom_call_target="tpu_custom_call" | custom-call | flops 4000000000 | bytes 2000000 | tf_op jit(solution)/shard_map/pallas_call | solution.py:235
  13.2 0.0 collective-permute-done.2
  13.3 1.5 %shard_map.39.third = f32[72,128]{1,0:T(8,128)S(1)} custom-call(f32[256,256]{1,0:T(8,128)S(1)} %bitcast.7, f32[3,144,512]{2,1,0:T(8,128)S(1)} %get-tuple-element.7.spec, f32[8,128]{1,0:T(8,128)S(1)} %get-tuple-element.8.spread, bf16[1024,512]{1,0:T(8,128)(2,1)S(1)} %copy-done.3), custom_call_target="tpu_custom_call" | custom-call | flops 4000000000 | bytes 2000000 | tf_op jit(solution)/shard_map/pallas_call | solution.py:235
  14.8 0.0 copy-start.1
  14.8 0.0 collective-permute-done
  14.8 0.6 %copy-done.1 = s32[1,3]{1,0:T(1,128)S(1)} copy-done((s32[1,3]{1,0:T(1,128)S(1)}, s32[1,3]{1,0:T(1,128)}, u32[]{:S(2)}) %copy-start.1) | copy-done | bytes 36
  15.5 2.1 %shard_map.40 = f32[1,3,9,1024]{3,2,1,0:T(8,128)S(1)} custom-call(s32[1,3]{1,0:T(1,128)S(1)} %copy-done.1, f32[256,256]{1,0:T(8,128)S(1)} %bitcast.5, f32[3,144,512]{2,1,0:T(8,128)S(1)} %get-tuple-element.7.spec, f32[8,128]{1,0:T(8,128)S(1)} %get-tuple-element.8.spread, bf16[1024,512]{1,0:T(8,128)(2,1)S(1)} %copy-done.3, f32[72,128]{1,0:T(8,128)S(1)} %shard_map.38.second, ...), custom_call_target="tpu_custom_call" | custom-call | flops 4000000000 | bytes 2000000 | tf_op jit(solution)/shard_map/pallas_call | solution.py:235
  17.5 0.8 %copy.4 = f32[1,3,9,1024]{3,0,2,1:T(1,128)} copy(f32[1,3,9,1024]{3,2,1,0:T(8,128)S(1)} %shard_map.40) | data formatting | bytes 221184 | tf_op jit(solution)/shard_map/pallas_call | solution.py:235
Async XLA Ops:
  0.0 10.2 %collective-permute-start.1 = (f32[1,256,256]{2,1,0:T(8,128)}, f32[1,256,256]{2,1,0:T(8,128)S(1)}, u32[]{:S(2)}, u32[]{:S(2)}) collective-permute-start(f32[1,256,256]{2,1,0:T(8,128)} %param.3), channel_id=1, source_target_pairs={{2,0},{3,1},{4,2},{5,3},{6,4},{7,5},{8,6},{9,7},{10,8},{11,9},{12,... | collective-permute-start | bytes 786440 | tf_op jit(solution)/shard_map/ppermute | solution.py:254
  2.1 12.7 %collective-permute-start = (f32[1,256,256]{2,1,0:T(8,128)}, f32[1,256,256]{2,1,0:T(8,128)S(1)}, u32[]{:S(2)}, u32[]{:S(2)}) collective-permute-start(f32[1,256,256]{2,1,0:T(8,128)} %param.3), channel_id=1, source_target_pairs={{1,0},{3,2},{4,1},{5,4},{6,3},{7,6},{8,5},{9,8},{10,7},{11,10},{12... | collective-permute-start | bytes 786440 | tf_op jit(solution)/shard_map/ppermute | solution.py:255
  5.0 1.0 %copy-start = (f32[1,256,256]{2,1,0:T(8,128)S(1)}, f32[1,256,256]{2,1,0:T(8,128)}, u32[]{:S(2)}) copy-start(f32[1,256,256]{2,1,0:T(8,128)} %param.3) | copy-start | bytes 786436
  6.0 1.2 %copy-start.2 = (bf16[1024,512]{1,0:T(8,128)(2,1)S(1)}, bf16[1024,512]{1,0:T(8,128)(2,1)}, u32[]{:S(2)}) copy-start(bf16[1024,512]{1,0:T(8,128)(2,1)} %constant.2.clone.packed) | copy-start | bytes 3145732
  7.2 4.5 %copy-start.3 = (bf16[1024,512]{1,0:T(8,128)(2,1)S(1)}, bf16[1024,512]{1,0:T(8,128)(2,1)}, u32[]{:S(2)}) copy-start(bf16[1024,512]{1,0:T(8,128)(2,1)} %constant.2.clone.packed) | copy-start | bytes 3145732
  10.2 3.1 %collective-permute-start.2 = (f32[1,256,256]{2,1,0:T(8,128)S(1)}, f32[1,256,256]{2,1,0:T(8,128)S(1)}, u32[]{:S(2)}, u32[]{:S(2)}) collective-permute-start(f32[1,256,256]{2,1,0:T(8,128)S(1)} %collective-permute-done.1), channel_id=1, source_target_pairs={{0,1},{1,0},{2,3},{3,2},{4,5},{5,4},{6,7},{7,6},{8,9},{9,8},{10,11... | collective-permute-start | bytes 786440 | tf_op jit(solution)/shard_map/ppermute | solution.py:256
  14.8 0.7 %copy-start.1 = (s32[1,3]{1,0:T(1,128)S(1)}, s32[1,3]{1,0:T(1,128)}, u32[]{:S(2)}) copy-start(s32[1,3]{1,0:T(1,128)} %partners.1) | copy-start | bytes 40
